TPU v7x, 32 devices: a whole 2x2x4 slice. The times are simulated.
32 devices in a mesh: row: 4 (over y, core), phi: 8 (over z, x).
Axes of the slice: x: 2, y: 2, z: 4, core: 2. Of those that a mesh axis runs over, the one named last changes fastest.
Arguments:
- hydro_vars: float32 [5, 128, 128, 256], P(None, 'row', 'phi'), may hold values from -6 to 6
- face_b: float32 [3, 128, 128, 256], P(None, 'row', 'phi'), may hold values from -6 to 6
- widths: int32 [16], replicated, may hold values from 2 to 128, as said below
- diffusion: float32 [5, 256], replicated, may hold values from 0.01 to 0.06
Outputs:
- conserved: float32 [8, 128, 128, 256], P(None, 'row', 'phi')
- faces_out: float32 [3, 128, 128, 256], P(None, 'row', 'phi')
Inputs may be any that keep to these rules, and one draw needn't show every extreme that they name: `widths`: every width is a power of two that divides 128; the two cycles next to the poles (entries 0 and 15) use 128.
All inputs are finite; a program needn't handle non-finite values.
Results may differ from a plain program's by a relative error of at most 0.0001.
Values sent between devices are 32-bit elements; how exact they have to be, the bound alone decides.
No kernel may reach another device: no remote copies, remote signals or barrier semaphores. Data moves between devices by JAX's collectives and lax.ppermute only.
A program may use at most 64 MiB of HBM per device.

v0:
```python
import jax
import jax.numpy as jnp
from jax import lax
from jax.sharding import PartitionSpec as P

CYCLES = 8


def extended(cells, sides, width, closed):
    for axis, dim in sides:
        count = lax.axis_size(axis)
        ends = count if closed else count - 1
        head = lax.slice_in_dim(cells, 0, width, axis=dim)
        tail = lax.slice_in_dim(cells, cells.shape[dim] - width, cells.shape[dim], axis=dim)
        cells = jnp.concatenate(
            [
                lax.ppermute(tail, axis, [(i, (i + 1) % count) for i in range(ends)]),
                cells,
                lax.ppermute(head, axis, [((i + 1) % count, i) for i in range(ends)]),
            ],
            axis=dim,
        )
    return cells


def passed_along(value, axis, steps):
    count = lax.axis_size(axis)
    initial, last = (max(0, -steps), min(count, count - steps))
    return lax.ppermute(value, axis, [(source, source + steps) for source in range(initial, last)])


def passed_along_2(block, axis, distance):
    devices = range(lax.axis_size(axis))
    route = [((i - distance) % len(devices), i) for i in devices]
    return lax.ppermute(block, axis, route)


def stencil(padded, axis, count):
    parts = [lax.slice_in_dim(padded, offset, offset + count, axis=axis) for offset in range(5)]
    return (16.0 * (parts[1] + parts[3]) - (parts[0] + parts[4]) - 30.0 * parts[2]) / 12.0


def block_means(cycles, axis, width, limit):
    cells = cycles.shape[axis]
    result = cycles
    for power in range(1, limit.bit_length()):
        size = 2**power
        shape = cycles.shape[:axis] + (cells // size, size) + cycles.shape[axis + 1 :]
        means = jnp.mean(cycles.reshape(shape), axis=axis + 1, keepdims=True)
        means = jnp.broadcast_to(means, shape).reshape(cycles.shape)
        result = jnp.where(width == size, means, result)
    return result


def body(hydro_vars, face_b, widths, diffusion):
    fields = jnp.concatenate([hydro_vars, face_b], 0)
    nfield, rows, cells, theta_cells = fields.shape
    cycle_count = 2 * CYCLES
    polar_cycles = jnp.concatenate([fields[..., :CYCLES], fields[..., theta_cells - CYCLES :]], 3)
    slab = polar_cycles.transpose(2, 0, 1, 3).reshape(cells, nfield * rows * cycle_count)
    whole = lax.all_to_all(slab, "phi", split_axis=1, concat_axis=0, tiled=True)
    columns = whole.shape[1]
    first = lax.axis_index("phi") * columns
    cycle_of = (first + jnp.arange(columns, dtype=jnp.int32)) % cycle_count
    match = cycle_of[:, None] == jnp.arange(cycle_count, dtype=jnp.int32)[None, :]
    column_width = jnp.sum(jnp.where(match, widths[None, :], 0), axis=1)
    means = block_means(whole, 0, column_width[None, :], whole.shape[0])
    back = lax.all_to_all(means, "phi", split_axis=0, concat_axis=1, tiled=True)
    averaged = back.reshape(cells, nfield, rows, cycle_count).transpose(1, 2, 0, 3)
    fields = jnp.concatenate(
        [
            averaged[..., :CYCLES],
            fields[..., CYCLES : theta_cells - CYCLES],
            averaged[..., CYCLES:],
        ],
        3,
    )
    hydro = fields[:5]
    radial_pad = extended(hydro, (("row", 1),), 2, False)
    azimuth_pad = extended(hydro, (("phi", 2),), 2, True)
    change_radial = stencil(radial_pad, 1, rows)
    change_azimuth = stencil(azimuth_pad, 2, cells)
    outer_layer = passed_along(fields[5, :1], "row", -1)
    radial_next = jnp.concatenate([fields[5, 1:], outer_layer], 0)
    after_layer = passed_along_2(fields[7, :, :1], "phi", -1)
    azimuth_next = jnp.concatenate([fields[7, :, 1:], after_layer], 1)
    theta_pad = jnp.pad(hydro, ((0, 0), (0, 0), (0, 0), (2, 2)))
    change = change_radial + change_azimuth + stencil(theta_pad, 3, theta_cells)
    smoothed = hydro + diffusion[:, None, None, :] * change
    polar_face = fields[6]
    polar_next = jnp.concatenate([polar_face[..., 1:], jnp.zeros_like(polar_face[..., :1])], 2)
    cell_field = 0.5 * jnp.stack(
        [fields[5] + radial_next, polar_face + polar_next, fields[7] + azimuth_next]
    )
    return (jnp.concatenate([smoothed, cell_field], 0), fields[5:])


def solution(mesh):
    in_specs = (P(None, "row", "phi", None), P(None, "row", "phi", None), P(), P())
    out_specs = (P(None, "row", "phi", None), P(None, "row", "phi", None))
    return jax.shard_map(body, mesh=mesh, in_specs=in_specs, out_specs=out_specs, check_vma=False)
```

profile of v0, /device:TPU:6, one launch (start us, length us, event | category | flops | bytes accessed | tf_op | source)
XLA Modules:
  0.0 83.4 jit_solution(16778632475743452020)
XLA Ops:
  0.6 0.0 copy-start.3
  0.6 2.1 %constant_dynamic-update-slice_fusion.1 = f32[8,32,16,256]{3,2,1,0:T(8,128)S(1)} fusion(f32[5,32,16,256]{3,2,1,0:T(8,128)} %param.4), kind=kLoop, calls=%fused_computation.65 | loop fusion | bytes 5242880
  2.7 0.1 copy-done.3
  2.8 0.1 constant_dynamic-update-slice_fusion
  2.9 0.0 copy-start.2
  3.0 0.7 fusion.27
  3.7 1.3 %copy-done.2 = f32[8,32,16,256]{3,2,1,0:T(8,128)} copy-done((f32[8,32,16,256]{3,2,1,0:T(8,128)}, f32[8,32,16,256]{3,2,1,0:T(8,128)S(1)}, u32[]{:S(2)}) %copy-start.2) | copy-done | bytes 4194328
  5.0 0.6 maximum_bitcast_fusion
  5.6 0.0 copy-start.5
  5.6 0.6 copy.46
  6.2 2.3 %reshape.192 = f32[16,8,512]{2,0,1:T(8,128)} reshape(f32[16,8,32,16]{3,2,0,1:T(8,128)S(1)} %copy.46) | data formatting | bytes 524288 | tf_op jit(solution)/shard_map/all_to_all | solution.py:61
  8.5 6.3 %all-to-all-start = ((f32[16,8,512]{2,0,1:T(8,128)}), f32[16,8,512]{2,0,1:T(8,128)S(1)}, u32[]{:S(2)}, u32[]{:S(2)}) async-start(f32[16,8,512]{2,0,1:T(8,128)} %reshape.192), calls=%async_computation | async-start | bytes 524288 | tf_op jit(solution)/shard_map/all_to_all | solution.py:61
  14.8 0.0 copy-done.5
  14.8 0.1 select_reduce_fusion
  14.9 8.2 %all-to-all-done = f32[16,8,512]{2,0,1:T(8,128)S(1)} async-done(((f32[16,8,512]{2,0,1:T(8,128)}), f32[16,8,512]{2,0,1:T(8,128)S(1)}, u32[]{:S(2)}, u32[]{:S(2)}) %all-to-all-start) | async-done | bytes 262176 | tf_op jit(solution)/shard_map/all_to_all | solution.py:61
  23.2 0.1 reshape.189
  23.4 0.1 reshape.187
  23.7 0.1 reduce_sum.83
  23.7 0.3 reduce_sum.85
  24.1 0.1 broadcast_in_dim.122
  24.2 0.2 reshape.190
  24.4 0.2 reduce_sum.84
  24.6 0.1 reshape.188
  24.7 0.8 %fusion.25 = f32[8,16,512]{2,1,0:T(8,128)} fusion(f32[8,16,512]{2,1,0:T(8,128)S(1)} %reshape.188, f32[8,16,512]{2,1,0:T(8,128)S(1)} %reshape.190, f32[8,512]{1,0:T(8,128)S(1)} %broadcast_multiply_fusion.3, f32[8,512]{1,0:T(8,128)S(1)} %broadcast_in_dim.113, f32[8,512]{1,0:T(8,128)S(1)} %broadcast_in_dim.109, f32[512]{0:T(512)S(1)} %broadcast_multiply_fusion.7, ...), kind=kLoop, calls=%fused_computation.53 | loop fusion | flops 458752 | bytes 1365504 | tf_op jit(solution)/shard_map/jit(_where)/select_n | solution.py:51
  25.6 4.2 %all-to-all-start.1 = ((f32[8,16,512]{2,1,0:T(8,128)}), f32[8,16,512]{2,1,0:T(8,128)S(1)}, u32[]{:S(2)}, u32[]{:S(2)}) async-start(f32[8,16,512]{2,1,0:T(8,128)} %fusion.25), calls=%async_computation.1 | async-start | bytes 524288 | tf_op jit(solution)/shard_map/all_to_all | solution.py:68
  29.8 5.3 %slice.140 = f32[8,32,16,240]{3,2,1,0:T(8,128)} slice(f32[8,32,16,256]{3,2,1,0:T(8,128)} %copy-done.2), slice={[0:8], [0:32], [0:16], [8:248]} | slice | bytes 7864320 | tf_op jit(solution)/shard_map/slice | solution.py:73
  35.1 0.0 copy-done.4
  35.1 2.7 %all-to-all-done.1 = f32[8,16,512]{2,1,0:T(8,128)S(1)} async-done(((f32[8,16,512]{2,1,0:T(8,128)}), f32[8,16,512]{2,1,0:T(8,128)S(1)}, u32[]{:S(2)}, u32[]{:S(2)}) %all-to-all-start.1) | async-done | bytes 262176 | tf_op jit(solution)/shard_map/all_to_all | solution.py:68
  37.8 0.2 copy.39
  37.9 0.7 reshape.191
  38.7 0.8 fusion.28
  39.4 1.2 %copy.40 = f32[8,32,16,8]{3,2,1,0:T(8,128)S(1)} copy(f32[8,32,16,8]{3,1,0,2:T(8,128)S(1)} %get-tuple-element.13) | data formatting | bytes 262144 | tf_op jit(solution)/shard_map/slice | solution.py:72
  40.6 0.0 copy-start
  40.6 1.2 %copy.41 = f32[8,32,16,8]{3,2,1,0:T(8,128)S(1)} copy(f32[8,32,16,8]{3,1,0,2:T(8,128)S(1)} %get-tuple-element.14) | data formatting | bytes 262144 | tf_op jit(solution)/shard_map/slice | solution.py:74
  41.8 1.0 %copy-done = f32[8,32,16,240]{3,2,1,0:T(8,128)S(1)} copy-done((f32[8,32,16,240]{3,2,1,0:T(8,128)S(1)}, f32[8,32,16,240]{3,2,1,0:T(8,128)}, u32[]{:S(2)}) %copy-start) | copy-done | bytes 3932184
  42.8 0.1 maximum_bitcast_fusion.2
  42.9 0.2 maximum_bitcast_fusion.1
  43.1 1.1 %pad_maximum_fusion.7 = (f32[5,32,2,256]{3,2,1,0:T(2,128)S(1)}, f32[5,32,2,256]{3,2,1,0:T(2,128)S(1)}) fusion(f32[8,32,16,8]{3,2,1,0:T(8,128)S(1)} %copy.41, f32[8,32,16,240]{3,2,1,0:T(8,128)S(1)} %copy-done, f32[8,32,16,8]{3,2,1,0:T(8,128)S(1)} %copy.40), kind=kLoop, calls=%fused_computation.48 | loop fusion | flops 327680 | bytes 4849664 | tf_op jit(solution)/shard_map/slice | solution.py:14
  44.2 1.7 %pad_maximum_fusion = f32[8,32,16,256]{3,2,1,0:T(8,128)S(1)} fusion(f32[8,32,16,8]{3,2,1,0:T(8,128)S(1)} %copy.41, f32[8,32,16,240]{3,2,1,0:T(8,128)S(1)} %copy-done, f32[8,32,16,8]{3,2,1,0:T(8,128)S(1)} %copy.40), kind=kLoop, calls=%fused_computation.4 | loop fusion | flops 2097152 | bytes 8388608 | tf_op jit(solution)/shard_map/concatenate | solution.py:70
  45.8 0.0 copy-start.1
  45.9 1.9 %collective-permute-start.4 = (f32[1,16,256]{2,1,0:T(8,128)S(1)}, f32[1,16,256]{2,1,0:T(8,128)S(1)}, u32[]{:S(2)}, u32[]{:S(2)}) collective-permute-start(f32[1,16,256]{2,1,0:T(8,128)S(1)} %maximum_bitcast_fusion.2), channel_id=1, source_target_pairs={{8,0},{16,8},{24,16},{9,1},{17,9},{25,17},{10,2},{18,10},{26,18},{... | collective-permute-start | bytes 49160 | tf_op jit(solution)/shard_map/ppermute | solution.py:29
  47.8 0.6 collective-permute-start.5
  48.4 0.2 pad_maximum_fusion.9
  48.7 1.3 %slice.157 = f32[3,32,16,256]{3,2,1,0:T(8,128)} slice(f32[8,32,16,256]{3,2,1,0:T(8,128)S(1)} %pad_maximum_fusion), slice={[5:8], [0:32], [0:16], [0:256]} | slice | bytes 3145728 | tf_op jit(solution)/shard_map/slice | solution.py:95
  50.0 2.1 %collective-permute-start = (f32[5,2,16,256]{3,2,1,0:T(8,128)S(1)}, f32[5,2,16,256]{3,2,1,0:T(8,128)S(1)}, u32[]{:S(2)}, u32[]{:S(2)}) collective-permute-start(f32[5,2,16,256]{3,2,1,0:T(8,128)S(1)} %get-tuple-element.6), channel_id=1, source_target_pairs={{0,8},{8,16},{16,24},{1,9},{9,17},{17,25},{2,10},{10,18},{18,26},{... | collective-permute-start | bytes 491528 | tf_op jit(solution)/shard_map/ppermute | solution.py:17
  52.1 3.4 %collective-permute-start.1 = (f32[5,2,16,256]{3,2,1,0:T(8,128)S(1)}, f32[5,2,16,256]{3,2,1,0:T(8,128)}, u32[]{:S(2)}, u32[]{:S(2)}) collective-permute-start(f32[5,2,16,256]{3,2,1,0:T(8,128)S(1)} %get-tuple-element.7), channel_id=1, source_target_pairs={{8,0},{16,8},{24,16},{9,1},{17,9},{25,17},{10,2},{18,10},{26,18},{... | collective-permute-start | bytes 491528 | tf_op jit(solution)/shard_map/ppermute | solution.py:19
  55.6 2.4 %collective-permute-start.3 = (f32[5,32,2,256]{3,1,2,0:T(8,128)S(1)}, f32[5,32,2,256]{3,1,2,0:T(8,128)S(1)}, u32[]{:S(2)}, u32[]{:S(2)}) collective-permute-start(f32[5,32,2,256]{3,1,2,0:T(8,128)S(1)} %copy.44), channel_id=1, source_target_pairs={{1,0},{2,1},{3,2},{4,3},{5,4},{6,5},{7,6},{0,7},{9,8},{10,9},{11,1... | collective-permute-start | bytes 983048 | tf_op jit(solution)/shard_map/ppermute | solution.py:19
  58.0 0.0 collective-permute-done.4
  58.0 0.6 collective-permute-start.2
  58.6 0.0 collective-permute-done.5
  58.6 0.3 slice_add_fusion.1
  58.9 0.2 slice.154
  59.1 0.1 add_bitcast_fusion
  59.2 0.0 slice-start
  59.2 0.2 maximum_multiply_fusion
  59.4 12.4 %collective-permute-done.3 = f32[5,32,2,256]{3,1,2,0:T(8,128)S(1)} collective-permute-done((f32[5,32,2,256]{3,1,2,0:T(8,128)S(1)}, f32[5,32,2,256]{3,1,2,0:T(8,128)S(1)}, u32[]{:S(2)}, u32[]{:S(2)}) %collective-permute-start.3) | collective-permute-done | bytes 327712 | tf_op jit(solution)/shard_map/ppermute | solution.py:19
  71.7 0.3 copy.45
  72.0 0.8 collective-permute-done.2
  72.8 0.3 copy.43
  73.1 0.0 collective-permute-done
  73.1 0.0 collective-permute-done.1
  73.1 0.0 slice-done
  73.1 6.1 %fusion.8 = f32[5,32,16,256]{3,2,1,0:T(8,128)} fusion(f32[5,32,16,256]{3,2,1,0:T(8,128)S(1)} %slice-done, f32[5,2,16,256]{3,2,1,0:T(8,128)} %collective-permute-done.1, f32[5,2,16,256]{3,2,1,0:T(8,128)S(1)} %collective-permute-done, f32[5,32,2,256]{3,2,1,0:T(2,128)S(1)} %copy.45, f32[5,32,2,256]{3,2,1,0:T(2,128)S(1)} %copy.43, ...), kind=kLoop, calls=%fused_computation.22 | loop fusion | flops 18350080 | bytes 6231040 | tf_op jit(solution)/shard_map/add | solution.py:89
  79.2 4.2 %pad_maximum_fusion.1 = f32[8,32,16,256]{3,2,1,0:T(8,128)} fusion(f32[3,32,16,256]{3,2,1,0:T(8,128)S(1)} %maximum_multiply_fusion, f32[5,32,16,256]{3,2,1,0:T(8,128)} %fusion.8), kind=kLoop, calls=%fused_computation.5 | loop fusion | flops 1048576 | bytes 8388608 | tf_op jit(solution)/shard_map/concatenate | solution.py:95
  (28 shorter events, 0.5 us)
Async XLA Ops:
  0.6 2.2 %copy-start.3 = (f32[3,32,16,256]{3,2,1,0:T(8,128)S(1)}, f32[3,32,16,256]{3,2,1,0:T(8,128)}, u32[]{:S(2)}) copy-start(f32[3,32,16,256]{3,2,1,0:T(8,128)} %param.5) | copy-start | bytes 4718596
  2.9 2.0 %copy-start.2 = (f32[8,32,16,256]{3,2,1,0:T(8,128)}, f32[8,32,16,256]{3,2,1,0:T(8,128)S(1)}, u32[]{:S(2)}) copy-start(f32[8,32,16,256]{3,2,1,0:T(8,128)S(1)} %constant_dynamic-update-slice_fusion) | copy-start | bytes 12582916
  5.6 9.3 %copy-start.5 = (s32[16]{0:T(128)S(1)}, s32[16]{0:T(128)}, u32[]{:S(2)}) copy-start(s32[16]{0:T(128)} %param.6) | copy-start | bytes 196
  8.5 14.6 %all-to-all-start = ((f32[16,8,512]{2,0,1:T(8,128)}), f32[16,8,512]{2,0,1:T(8,128)S(1)}, u32[]{:S(2)}, u32[]{:S(2)}) async-start(f32[16,8,512]{2,0,1:T(8,128)} %reshape.192), calls=%async_computation | async-start | bytes 524288 | tf_op jit(solution)/shard_map/all_to_all | solution.py:61
  25.6 12.2 %all-to-all-start.1 = ((f32[8,16,512]{2,1,0:T(8,128)}), f32[8,16,512]{2,1,0:T(8,128)S(1)}, u32[]{:S(2)}, u32[]{:S(2)}) async-start(f32[8,16,512]{2,1,0:T(8,128)} %fusion.25), calls=%async_computation.1 | async-start | bytes 524288 | tf_op jit(solution)/shard_map/all_to_all | solution.py:68
  29.8 5.3 %copy-start.4 = (f32[5,256]{1,0:T(8,128)S(1)}, f32[5,256]{1,0:T(8,128)}, u32[]{:S(2)}) copy-start(f32[5,256]{1,0:T(8,128)} %param.7) | copy-start | bytes 15364
  40.6 2.2 %copy-start = (f32[8,32,16,240]{3,2,1,0:T(8,128)S(1)}, f32[8,32,16,240]{3,2,1,0:T(8,128)}, u32[]{:S(2)}) copy-start(f32[8,32,16,240]{3,2,1,0:T(8,128)} %slice.140) | copy-start | bytes 11796484
  45.8 13.2 %copy-start.1 = (f32[8,32,16,256]{3,2,1,0:T(8,128)}, f32[8,32,16,256]{3,2,1,0:T(8,128)S(1)}, u32[]{:S(2)}) copy-start(f32[8,32,16,256]{3,2,1,0:T(8,128)S(1)} %pad_maximum_fusion) | copy-start | bytes 12582916
  45.9 12.1 %collective-permute-start.4 = (f32[1,16,256]{2,1,0:T(8,128)S(1)}, f32[1,16,256]{2,1,0:T(8,128)S(1)}, u32[]{:S(2)}, u32[]{:S(2)}) collective-permute-start(f32[1,16,256]{2,1,0:T(8,128)S(1)} %maximum_bitcast_fusion.2), channel_id=1, source_target_pairs={{8,0},{16,8},{24,16},{9,1},{17,9},{25,17},{10,2},{18,10},{26,18},{... | collective-permute-start | bytes 49160 | tf_op jit(solution)/shard_map/ppermute | solution.py:29
  47.8 10.8 %collective-permute-start.5 = (f32[32,1,256]{2,1,0:T(1,128)S(1)}, f32[32,1,256]{2,1,0:T(1,128)S(1)}, u32[]{:S(2)}, u32[]{:S(2)}) collective-permute-start(f32[32,1,256]{2,1,0:T(1,128)S(1)} %maximum_bitcast_fusion.1), channel_id=1, source_target_pairs={{1,0},{2,1},{3,2},{4,3},{5,4},{6,5},{7,6},{0,7},{9,8},{10,9},{11,1... | collective-permute-start | bytes 98312 | tf_op jit(solution)/shard_map/ppermute | solution.py:35
  50.0 23.1 %collective-permute-start = (f32[5,2,16,256]{3,2,1,0:T(8,128)S(1)}, f32[5,2,16,256]{3,2,1,0:T(8,128)S(1)}, u32[]{:S(2)}, u32[]{:S(2)}) collective-permute-start(f32[5,2,16,256]{3,2,1,0:T(8,128)S(1)} %get-tuple-element.6), channel_id=1, source_target_pairs={{0,8},{8,16},{16,24},{1,9},{9,17},{17,25},{2,10},{10,18},{18,26},{... | collective-permute-start | bytes 491528 | tf_op jit(solution)/shard_map/ppermute | solution.py:17
  52.1 21.0 %collective-permute-start.1 = (f32[5,2,16,256]{3,2,1,0:T(8,128)S(1)}, f32[5,2,16,256]{3,2,1,0:T(8,128)}, u32[]{:S(2)}, u32[]{:S(2)}) collective-permute-start(f32[5,2,16,256]{3,2,1,0:T(8,128)S(1)} %get-tuple-element.7), channel_id=1, source_target_pairs={{8,0},{16,8},{24,16},{9,1},{17,9},{25,17},{10,2},{18,10},{26,18},{... | collective-permute-start | bytes 491528 | tf_op jit(solution)/shard_map/ppermute | solution.py:19
  55.6 16.2 %collective-permute-start.3 = (f32[5,32,2,256]{3,1,2,0:T(8,128)S(1)}, f32[5,32,2,256]{3,1,2,0:T(8,128)S(1)}, u32[]{:S(2)}, u32[]{:S(2)}) collective-permute-start(f32[5,32,2,256]{3,1,2,0:T(8,128)S(1)} %copy.44), channel_id=1, source_target_pairs={{1,0},{2,1},{3,2},{4,3},{5,4},{6,5},{7,6},{0,7},{9,8},{10,9},{11,1... | collective-permute-start | bytes 983048 | tf_op jit(solution)/shard_map/ppermute | solution.py:19
  58.0 14.9 %collective-permute-start.2 = (f32[5,32,2,256]{3,1,2,0:T(8,128)S(1)}, f32[5,32,2,256]{3,1,2,0:T(8,128)S(1)}, u32[]{:S(2)}, u32[]{:S(2)}) collective-permute-start(f32[5,32,2,256]{3,1,2,0:T(8,128)S(1)} %copy.42), channel_id=1, source_target_pairs={{0,1},{1,2},{2,3},{3,4},{4,5},{5,6},{6,7},{7,0},{8,9},{9,10},{10,1... | collective-permute-start | bytes 983048 | tf_op jit(solution)/shard_map/ppermute | solution.py:17
  59.2 13.9 %slice-start = ((f32[8,32,16,256]{3,2,1,0:T(8,128)}), f32[5,32,16,256]{3,2,1,0:T(8,128)S(1)}, s32[]{:S(2)}) async-start(f32[8,32,16,256]{3,2,1,0:T(8,128)} %copy-done.1), calls=%async_computation.2 | async-start | bytes 5242880 | tf_op jit(solution)/shard_map/slice | solution.py:78
where the time goes:
time: 85 us; the launch traced here: 83.4 us
  waiting for transfers between devices  24.1 us (28%)
  starting transfers between devices  21.6 us (25%)
  local copies, waits for them, and re-layouts  20.3 us (24%)
  other arithmetic  16.3 us (19%)
  between operations  1.07 us (1%)
    ppermute x2, waiting for transfers between devices, extended(): lax.ppermute(head, axis, [((i + 1) % count, i) for i in range(ends)])  12.4 us
    all_to_all x1, waiting for transfers between devices, body(): whole = lax.all_to_all(slab, 'phi', split_axis=1, concat_axis=0, tiled=True)  8.19 us
    all_to_all x1, starting transfers between devices, body(): whole = lax.all_to_all(slab, 'phi', split_axis=1, concat_axis=0, tiled=True)  6.34 us
    add x1, other arithmetic, body(): smoothed = hydro + diffusion[:, None, None, :] * change  6.07 us
    ppermute x2, starting transfers between devices, extended(): lax.ppermute(head, axis, [((i + 1) % count, i) for i in range(ends)])  5.8 us
    slice x1, local copies, waits for them, and re-layouts, body(): fields[..., CYCLES:theta_cells - CYCLES]  5.28 us
    unnamed x13, local copies, waits for them, and re-layouts  4.44 us
    concatenate x1, other arithmetic, body(): return (jnp.concatenate([smoothed, cell_field], 0), fields[5:])  4.2 us
  transfers between devices with their start and end apart: 8, of which 4 were waited for; matrix products, arithmetic and copies ran while one was open for 10% of the time, Pallas kernels for 0%

commit v1 on v0

v1 whole, which is shorter than its diff:
```python
import functools

import jax
import jax.numpy as jnp
from jax import lax
from jax.experimental import pallas as pl
from jax.experimental.pallas import tpu as pltpu
from jax.sharding import PartitionSpec as P

CYCLES = 8
HYDRO = 5
FIELDS = 8
LANES = 128
SLOTS = 2 * CYCLES
F32 = jnp.float32
ANY = pl.BlockSpec(memory_space=pl.ANY)
VMEM = pl.BlockSpec(memory_space=pltpu.VMEM)


def lane_index(shape):
    return lax.broadcasted_iota(jnp.int32, shape, len(shape) - 1)


def lane_widths(widths):
    slot = lane_index((1, LANES)) % SLOTS
    row = jnp.zeros((1, LANES), jnp.int32)
    for s in range(SLOTS):
        row = jnp.where(slot == s, widths[(s + CYCLES) % SLOTS], row)
    return row


def packed_shift(field):
    return (SLOTS * field + CYCLES) % LANES


def unpack(field, packed):
    return pltpu.roll(packed, (LANES - packed_shift(field)) % LANES, packed.ndim - 1)


def merge(field, spread, values, tile, tiles):
    lane = lane_index(values.shape)
    if tile == 0:
        values = jnp.where(lane < CYCLES, spread, values)
    if tile == tiles - 1:
        values = jnp.where(lane >= LANES - CYCLES, spread, values)
    return values


def lanes_of(tile):
    return slice(tile * LANES, (tile + 1) * LANES)


def with_polar(field, packed, values):
    tiles = values.shape[-1] // LANES
    spread = unpack(field, packed)
    parts = [merge(field, spread, values[..., lanes_of(t)], t, tiles) for t in range(tiles)]
    return jnp.concatenate(parts, values.ndim - 1)


def load_fields(h, b, buf, sems):
    copies = []
    for f in range(FIELDS):
        source = h.at[f] if f < HYDRO else b.at[f - HYDRO]
        copies.append([])
        for t in range(buf.shape[1]):
            copies[f].append(pltpu.make_async_copy(source.at[:, lanes_of(t)], buf.at[f, t], sems.at[f, t]))
    for field in copies:
        for copy in field:
            copy.start()
    return copies


def local_kernel(rows, cells, h, b, w, d, q, m, fw, bw, buf, pack, dv, wsm, sems, isems):
    tiles = buf.shape[1]
    size = rows * cells
    small = [pltpu.make_async_copy(w, wsm, sems.at[0]), pltpu.make_async_copy(d, dv, sems.at[1])]
    for copy in small:
        copy.start()
    copies = load_fields(h, b, buf, isems)
    small[0].wait()
    wl = lane_widths(wsm)
    lane = lane_index((size, LANES))
    for f in range(FIELDS):
        for copy in copies[f]:
            copy.wait()
        both = jnp.where(lane < CYCLES, buf[f, 0], buf[f, tiles - 1])
        spread = pltpu.roll(both, packed_shift(f), 1)
        pack[...] = spread if f == 0 else jnp.where(lane // SLOTS == f, spread, pack[...])
    cur = pack[...].reshape(size // 8, 8, LANES)
    result = cur
    place = lax.broadcasted_iota(jnp.int32, cur.shape, 1)
    span = 1
    while span < 8:
        other = jnp.where(place & span == 0, pltpu.roll(cur, 8 - span, 1), pltpu.roll(cur, span, 1))
        cur = cur + other
        span *= 2
        result = jnp.where(wl[None] == span, cur * (1.0 / span), result)
    cur = cur.reshape(rows, cells // 8, 8, LANES)
    while span < cells:
        group = span // 8
        parts = cur.reshape(rows, cells // (2 * span), 2, group, 8, LANES)
        both = parts[:, :, 0] + parts[:, :, 1]
        cur = jnp.stack([both, both], 2).reshape(cur.shape)
        span *= 2
        result = jnp.where(wl[None] == span, cur.reshape(result.shape) * (1.0 / span), result)
    spread = cur.reshape(result.shape) * (1.0 / cells)
    result = jnp.where(wl[None] >= cells, spread, result)
    q[...] = result.reshape(size, LANES)
    pack[...] = spread.reshape(size, LANES)
    m[...] = pack[pl.ds(0, rows, stride=cells), :]
    small[1].wait()

    def edge(f, cell):
        packed = jnp.where(wl >= 2 * cells, 0.0, q[pl.ds(cell, rows, stride=cells), :])
        spread = unpack(f, packed)
        return [merge(f, spread, buf[f, t, pl.ds(cell, rows, stride=cells), :], t, tiles) for t in range(tiles)]

    for f in range(HYDRO):
        for target, close, past in ((fw, cells - 1, cells - 2), (bw, 0, 1)):
            near, far = edge(f, close), edge(f, past)
            for t in range(tiles):
                scale = dv[f : f + 1, lanes_of(t)] * (1.0 / 12.0)
                target[2 * f, :, lanes_of(t)] = scale * (16.0 * near[t] - far[t])
                target[2 * f + 1, :, lanes_of(t)] = -scale * near[t]
    near = edge(FIELDS - 1, 0)
    for t in range(tiles):
        bw[2 * HYDRO, :, lanes_of(t)] = 0.5 * near[t]


def row_kernel(rows, cells, axis, h, b, w, d, g, q, mself, mout, up, dn, low, high, face, dv, wsm, sems):
    copies = [
        pltpu.make_async_copy(w, wsm, sems.at[0]),
        pltpu.make_async_copy(d, dv, sems.at[1]),
        pltpu.make_async_copy(h.at[:, pl.ds(0, 2 * cells), :], low, sems.at[2]),
        pltpu.make_async_copy(h.at[:, pl.ds((rows - 2) * cells, 2 * cells), :], high, sems.at[3]),
        pltpu.make_async_copy(b.at[0, pl.ds(0, cells), :], face, sems.at[4]),
    ]
    for copy in copies:
        copy.start()
    copies[0].wait()
    wl = lane_widths(wsm)
    pairs = g.shape[0]
    me = lax.axis_index(axis)
    mine = me // 2
    outer = jnp.where(me % 2 == 0, mine + pairs - 1, mine + 1) % pairs
    apart = mine ^ outer
    span, own, total_own, taken = 1, jnp.zeros(mself.shape, F32), jnp.zeros(mself.shape, F32), 0
    far = jnp.zeros(mself.shape, F32)
    while span <= pairs:
        for i in range(taken, span):
            total_own = total_own + g[i]
        taken = span
        start = (apart // span) * span
        total_far = g[start]
        for i in range(1, span):
            total_far = total_far + g[start + i]
        hit = wl == 2 * cells * span
        own = jnp.where(hit, total_own * (1.0 / span), own)
        far = jnp.where(hit, total_far * (1.0 / span), far)
        span *= 2
    mself[...] = own
    mout[...] = far
    for copy in copies[1:]:
        copy.wait()

    def polar_row(r):
        local = q[r * cells : (r + 1) * cells, :]
        return jnp.where(wl >= 2 * cells, jnp.broadcast_to(own[r : r + 1, :], local.shape), local)

    top, below = polar_row(rows - 1), polar_row(rows - 2)
    first, second = polar_row(0), polar_row(1)
    for f in range(HYDRO):
        scale = dv[f : f + 1, :] * (1.0 / 12.0)
        near, past = with_polar(f, top, high[f, cells:, :]), with_polar(f, below, high[f, :cells, :])
        up[2 * f] = scale * (16.0 * near - past)
        up[2 * f + 1] = -scale * near
        near, past = with_polar(f, first, low[f, :cells, :]), with_polar(f, second, low[f, cells:, :])
        dn[2 * f] = scale * (16.0 * near - past)
        dn[2 * f + 1] = -scale * near
    dn[2 * HYDRO] = 0.5 * with_polar(HYDRO, first, face[...])


def lane_shift(parts, by):
    lane = lane_index(parts[0].shape)
    rolled = [pltpu.roll(part, by % LANES, 1) for part in parts]
    zero = jnp.zeros_like(parts[0])
    if by > 0:
        return [jnp.where(lane < by, rolled[t - 1] if t > 0 else zero, rolled[t]) for t in range(len(parts))]
    after = rolled[1:] + [zero]
    return [jnp.where(lane >= LANES + by, after[t], rolled[t]) for t in range(len(parts))]


def cell_shift(part, by):
    cells = part.shape[0]
    place = lax.broadcasted_iota(jnp.int32, part.shape, 0)
    inside = place >= by if by > 0 else place < cells + by
    return jnp.where(inside, pltpu.roll(part, by % cells, 0), 0.0)


def main_kernel(rows, cells, axis, h, b, w, d, q, mself, mout, up, dn, cons, faces, e, buf, pad, pol, cell, dv, wsm, sems, isems, osems):
    tiles = buf.shape[1]
    size = rows * cells
    small = [pltpu.make_async_copy(w, wsm, sems.at[0]), pltpu.make_async_copy(d, dv, sems.at[1])]
    for copy in small:
        copy.start()
    copies = load_fields(h, b, buf, isems)
    for copy in small:
        copy.wait()
    wl = lane_widths(wsm)
    wide = wl >= 2 * cells
    spread = jnp.broadcast_to(mself[...][:, None, :], (rows, cells, LANES)).reshape(size, LANES)
    pol[...] = jnp.where(wide, spread, q[...])
    even = lax.axis_index(axis) % 2 == 0
    left = jnp.where(wide, jnp.where(even, mout[...], mself[...]), 0.0)
    right = jnp.where(wide, jnp.where(even, mself[...], mout[...]), 0.0)
    pad[:, 0 : 2 * cells, :] = jnp.zeros((tiles, 2 * cells, LANES), F32)
    pad[:, 2 * cells + size :, :] = jnp.zeros((tiles, 2 * cells, LANES), F32)
    outs = []

    def put(source, target, sem):
        for t in range(tiles):
            outs.append(pltpu.make_async_copy(source.at[t], target.at[:, lanes_of(t)], sem.at[t]))
            outs[-1].start()

    def edge(f, cell_of, ref):
        return [ref[f, t, pl.ds(cell_of, rows, stride=cells), :] for t in range(tiles)]

    def polar_part(f, packed):
        spread = unpack(f, packed)
        return [merge(f, spread, jnp.zeros(spread.shape, F32), t, tiles) for t in range(tiles)]

    for f in range(HYDRO):
        for copy in copies[f]:
            copy.wait()
        spread = unpack(f, pol[...])
        for t in range(tiles):
            pad[t, 2 * cells : 2 * cells + size, :] = merge(f, spread, buf[f, t], t, tiles)
        scales = [dv[f : f + 1, lanes_of(t)] * (1.0 / 12.0) for t in range(tiles)]

        def step(r, carry):
            base = pl.multiple_of(r * cells, cells)
            v = [pad[t, pl.ds(base + 2 * cells, cells), :] for t in range(tiles)]
            before, after = lane_shift(v, 1), lane_shift(v, -1)
            before2, after2 = lane_shift(v, 2), lane_shift(v, -2)
            for t in range(tiles):
                one = pad[t, pl.ds(base + cells, cells), :] + pad[t, pl.ds(base + 3 * cells, cells), :]
                two = pad[t, pl.ds(base, cells), :] + pad[t, pl.ds(base + 4 * cells, cells), :]
                one = one + before[t] + after[t] + cell_shift(v[t], 1) + cell_shift(v[t], -1)
                two = two + before2[t] + after2[t] + cell_shift(v[t], 2) + cell_shift(v[t], -2)
                buf[f, t, pl.ds(base, cells), :] = v[t] + scales[t] * (16.0 * one - two - 90.0 * v[t])
            return carry

        lax.fori_loop(0, rows, step, 0, unroll=2)
        near, far = polar_part(f, left), polar_part(f, right)
        for t in range(tiles):
            buf[f, t, 0:cells, :] += up[2 * f, :, lanes_of(t)]
            buf[f, t, cells : 2 * cells, :] += up[2 * f + 1, :, lanes_of(t)]
            buf[f, t, size - cells :, :] += dn[2 * f, :, lanes_of(t)]
            buf[f, t, size - 2 * cells : size - cells, :] += dn[2 * f + 1, :, lanes_of(t)]
        for j, (cell_of, polar, factor) in enumerate(((0, near, 15.0), (1, near, -1.0), (cells - 1, far, 15.0), (cells - 2, far, -1.0))):
            own = edge(f, cell_of, buf)
            for t in range(tiles):
                e[4 * f + j, :, lanes_of(t)] = own[t] + (factor * scales[t]) * polar[t]
        put(buf.at[f], cons.at[f], osems.at[f])
    for k in range(FIELDS - HYDRO):
        f = HYDRO + k
        for copy in copies[f]:
            copy.wait()
        spread = unpack(f, pol[...])
        for t in range(tiles):
            buf[f, t] = merge(f, spread, buf[f, t], t, tiles)
        put(buf.at[f], faces.at[k], osems.at[FIELDS + k])
        if k == 0:
            for t in range(tiles):
                cell[k, t, : size - cells, :] = 0.5 * (buf[f, t, : size - cells, :] + buf[f, t, cells:, :])
                cell[k, t, size - cells :, :] = 0.5 * buf[f, t, size - cells :, :] + dn[2 * HYDRO, :, lanes_of(t)]
        else:

            def step(r, carry):
                base = pl.multiple_of(r * cells, cells)
                v = [buf[f, t, pl.ds(base, cells), :] for t in range(tiles)]
                after = lane_shift(v, -1) if k == 1 else [cell_shift(part, -1) for part in v]
                for t in range(tiles):
                    cell[k, t, pl.ds(base, cells), :] = 0.5 * (v[t] + after[t])
                return carry

            lax.fori_loop(0, rows, step, 0, unroll=2)
        if k == 2:
            own, far = edge(k, cells - 1, cell), polar_part(f, right)
            for t in range(tiles):
                e[4 * HYDRO, :, lanes_of(t)] = own[t] + 0.5 * far[t]
        put(cell.at[k], cons.at[f], osems.at[f])
    for copy in outs:
        copy.wait()


def edge_kernel(rows, cells, cons_in, e, fw, bw, cons, done, sems):
    del cons_in
    copies = []
    places = (0, 1, cells - 1, cells - 2)
    for f in range(HYDRO):
        for j in range(2):
            done[4 * f + j] = e[4 * f + j] + fw[2 * f + j]
            done[4 * f + 2 + j] = e[4 * f + 2 + j] + bw[2 * f + j]
        for j in range(4):
            copies.append(pltpu.make_async_copy(done.at[4 * f + j], cons.at[f, :, places[j], :], sems.at[4 * f + j]))
            copies[-1].start()
    done[4 * HYDRO] = e[4 * HYDRO] + bw[2 * HYDRO]
    copies.append(pltpu.make_async_copy(done.at[4 * HYDRO], cons.at[FIELDS - 1, :, cells - 1, :], sems.at[4 * HYDRO]))
    copies[-1].start()
    for copy in copies:
        copy.wait()


def params(mib):
    return pltpu.CompilerParams(vmem_limit_bytes=mib * 1024 * 1024)


def cost(flops, size):
    return pl.CostEstimate(flops=flops, bytes_accessed=size, transcendentals=0)


def body(hydro_vars, face_b, widths, diffusion):
    _, rows, cells, total = hydro_vars.shape
    size = rows * cells
    tiles = total // LANES
    count = lax.axis_size("phi")
    layers = lax.axis_size("row")
    h = hydro_vars.reshape(HYDRO, size, total)
    b = face_b.reshape(FIELDS - HYDRO, size, total)
    dma = pltpu.SemaphoreType.DMA

    def shape(*dims):
        return jax.ShapeDtypeStruct(dims, F32)

    q, m, fw, bw = pl.pallas_call(
        functools.partial(local_kernel, rows, cells),
        out_shape=[shape(size, LANES), shape(rows, LANES), shape(2 * HYDRO, rows, total), shape(2 * HYDRO + 1, rows, total)],
        in_specs=[ANY] * 4,
        out_specs=[VMEM] * 4,
        scratch_shapes=[
            pltpu.VMEM((FIELDS, tiles, size, LANES), F32),
            pltpu.VMEM((size, LANES), F32),
            pltpu.VMEM((HYDRO, total), F32),
            pltpu.SMEM((SLOTS,), jnp.int32),
            dma((2,)),
            dma((FIELDS, tiles)),
        ],
        compiler_params=params(12),
        cost_estimate=cost(5_000_000, 5_000_000),
        name="local",
    )(h, b, widths, diffusion)

    pair = lax.ppermute(m, "phi", [(i, i ^ 1) for i in range(count)])
    fw = lax.ppermute(fw, "phi", [(i, (i + 1) % count) for i in range(count)])
    bw = lax.ppermute(bw, "phi", [((i + 1) % count, i) for i in range(count)])
    g = (0.5 * (m + pair))[None]
    step = 2
    while step < count:
        g = jnp.concatenate([g, lax.ppermute(g, "phi", [(i, i ^ step) for i in range(count)])], 0)
        step *= 2

    mself, mout, up, dn = pl.pallas_call(
        functools.partial(row_kernel, rows, cells, "phi"),
        out_shape=[shape(rows, LANES), shape(rows, LANES), shape(2 * HYDRO, cells, total), shape(2 * HYDRO + 1, cells, total)],
        in_specs=[ANY] * 4 + [VMEM] * 2,
        out_specs=[VMEM] * 4,
        scratch_shapes=[
            pltpu.VMEM((HYDRO, 2 * cells, total), F32),
            pltpu.VMEM((HYDRO, 2 * cells, total), F32),
            pltpu.VMEM((cells, total), F32),
            pltpu.VMEM((HYDRO, total), F32),
            pltpu.SMEM((SLOTS,), jnp.int32),
            dma((5,)),
        ],
        compiler_params=params(8),
        cost_estimate=cost(2_000_000, 1_000_000),
        name="rows",
    )(h, b, widths, diffusion, g, q)
    up = lax.ppermute(up, "row", [(i, i + 1) for i in range(layers - 1)])
    dn = lax.ppermute(dn, "row", [(i + 1, i) for i in range(layers - 1)])

    cons, faces, e = pl.pallas_call(
        functools.partial(main_kernel, rows, cells, "phi"),
        out_shape=[shape(FIELDS, size, total), shape(FIELDS - HYDRO, size, total), shape(4 * HYDRO + 1, rows, total)],
        in_specs=[ANY] * 4 + [VMEM] * 5,
        out_specs=[ANY, ANY, VMEM],
        scratch_shapes=[
            pltpu.VMEM((FIELDS, tiles, size, LANES), F32),
            pltpu.VMEM((tiles, size + 4 * cells, LANES), F32),
            pltpu.VMEM((size, LANES), F32),
            pltpu.VMEM((FIELDS - HYDRO, tiles, size, LANES), F32),
            pltpu.VMEM((HYDRO, total), F32),
            pltpu.SMEM((SLOTS,), jnp.int32),
            dma((2,)),
            dma((FIELDS, tiles)),
            dma((2 * FIELDS - HYDRO, tiles)),
        ],
        compiler_params=params(16),
        cost_estimate=cost(20_000_000, 10_000_000),
        name="main",
    )(h, b, widths, diffusion, q, mself, mout, up, dn)

    cons = pl.pallas_call(
        functools.partial(edge_kernel, rows, cells),
        out_shape=shape(FIELDS, rows, cells, total),
        in_specs=[ANY] + [VMEM] * 3,
        out_specs=ANY,
        scratch_shapes=[pltpu.VMEM((4 * HYDRO + 1, rows, total), F32), dma((4 * HYDRO + 1,))],
        input_output_aliases={0: 0},
        compiler_params=params(8),
        cost_estimate=cost(1_000_000, 1_000_000),
        name="edges",
    )(cons.reshape(FIELDS, rows, cells, total), e, fw, bw)
    return cons, faces.reshape(FIELDS - HYDRO, rows, cells, total)


def solution(mesh):
    in_specs = (P(None, "row", "phi", None), P(None, "row", "phi", None), P(), P())
    out_specs = (P(None, "row", "phi", None), P(None, "row", "phi", None))
    return jax.shard_map(body, mesh=mesh, in_specs=in_specs, out_specs=out_specs, check_vma=False)
```

time: 85 us -> 51.1 us (0.60); the launches traced: 83.4 us -> 50.8 us
  Pallas kernels: 0 us -> 17.5 us
  other arithmetic: 16.3 us -> 0.01 us
  local copies, waits for them, and re-layouts: 20.3 us -> 4.52 us
  starting transfers between devices: 21.6 us -> 11.2 us
  waiting for transfers between devices: 24.1 us -> 16.9 us
    pallas_call x0 -> x4, Pallas kernels: none -> 17.5 us  [the longest x1 13.5 us: body(): pl.pallas_call(functools.partial(main_kernel, rows, cells, 'phi'), out_sh...]
    all_to_all x2 -> x0, waiting for transfers between devices: 10.9 us -> none  [the longest x1 8.19 us: body(): whole = lax.all_to_all(slab, 'phi', split_axis=1, concat_axis=0, tiled=True)]
    slice x13 -> x0, local copies, waits for them, and re-layouts: 10.8 us -> none  [the longest x1 5.28 us: body(): fields[..., CYCLES:theta_cells - CYCLES]]
    all_to_all x2 -> x0, starting transfers between devices: 10.5 us -> none  [the longest x1 6.34 us: body(): whole = lax.all_to_all(slab, 'phi', split_axis=1, concat_axis=0, tiled=True)]
    add x2 -> x0, other arithmetic: 6.37 us -> none  [the longest x1 6.07 us: body(): smoothed = hydro + diffusion[:, None, None, :] * change]
    concatenate x2, other arithmetic: 5.88 us -> 0.01 us  [body(): jnp.concatenate([g, lax.ppermute(g, 'phi', [(i, i ^ step) for i in range(...]
    ppermute x6 -> x7, waiting for transfers between devices: 13.2 us -> 16.9 us  [the longest x2 9.42 us: body(): lax.ppermute(g, 'phi', [(i, i ^ step) for i in range(count)])]
    all_to_all x3 -> x0, local copies, waits for them, and re-layouts: 3.04 us -> none  [the longest x2 2.89 us: body(): whole = lax.all_to_all(slab, 'phi', split_axis=1, concat_axis=0, tiled=True)]
  transfers between devices with their start and end apart: 8 -> 7, of which waited for: 4 -> 4; matrix products, arithmetic and copies ran while one was open for 10% -> 0% of each run, Pallas kernels for 0% -> 28%
where the time goes in v1:
time: 51.1 us; the launch traced here: 50.8 us
  Pallas kernels  17.5 us (34%)
  waiting for transfers between devices  16.9 us (33%)
  starting transfers between devices  11.2 us (22%)
  local copies, waits for them, and re-layouts  4.52 us (9%)
  between operations  0.74 us (1%)
    pallas_call x1, Pallas kernels, body(): pl.pallas_call(functools.partial(main_kernel, rows, cells, 'phi'), out_sh...  13.5 us
    ppermute x2, waiting for transfers between devices, body(): lax.ppermute(g, 'phi', [(i, i ^ step) for i in range(count)])  9.42 us
    unnamed x16, local copies, waits for them, and re-layouts  4.52 us
    ppermute x1, waiting for transfers between devices, body(): up = lax.ppermute(up, 'row', [(i, i + 1) for i in range(layers - 1)])  4.22 us
    ppermute x2, starting transfers between devices, body(): lax.ppermute(g, 'phi', [(i, i ^ step) for i in range(count)])  4.17 us
    ppermute x1, waiting for transfers between devices, body(): pair = lax.ppermute(m, 'phi', [(i, i ^ 1) for i in range(count)])  3.2 us
    ppermute x1, starting transfers between devices, body(): up = lax.ppermute(up, 'row', [(i, i + 1) for i in range(layers - 1)])  2.41 us
    pallas_call x1, Pallas kernels, body(): pl.pallas_call(functools.partial(local_kernel, rows, cells), out_shape=[s...  2.24 us
  transfers between devices with their start and end apart: 7, of which 4 were waited for; matrix products, arithmetic and copies ran while one was open for 0% of the time, Pallas kernels for 28%

profile of v1, /device:TPU:6, one launch (start us, length us, event | category | flops | bytes accessed | tf_op | source)
XLA Modules:
  0.0 50.8 jit_solution(14257014624949123415)
XLA Ops:
  0.6 0.0 copy-start.7
  0.6 0.0 copy-start
  0.6 1.7 %copy-done = f32[5,32,16,256]{3,2,1,0:T(8,128)S(1)} copy-done((f32[5,32,16,256]{3,2,1,0:T(8,128)S(1)}, f32[5,32,16,256]{3,2,1,0:T(8,128)}, u32[]{:S(2)}) %copy-start) | copy-done | bytes 2621464
  2.4 0.0 copy-start.2
  2.4 1.4 %copy-done.2 = f32[3,32,16,256]{3,2,1,0:T(8,128)S(1)} copy-done((f32[3,32,16,256]{3,2,1,0:T(8,128)S(1)}, f32[3,32,16,256]{3,2,1,0:T(8,128)}, u32[]{:S(2)}) %copy-start.2) | copy-done | bytes 1572888
  3.8 0.0 copy-start.4
  3.8 0.7 %copy-done.4 = f32[5,256]{1,0:T(8,128)S(1)} copy-done((f32[5,256]{1,0:T(8,128)S(1)}, f32[5,256]{1,0:T(8,128)}, u32[]{:S(2)}) %copy-start.4) | copy-done | bytes 5144
  4.5 0.0 copy-start.6
  4.5 0.7 %copy-done.6 = s32[16]{0:T(128)S(1)} copy-done((s32[16]{0:T(128)S(1)}, s32[16]{0:T(128)}, u32[]{:S(2)}) %copy-start.6) | copy-done | bytes 88
  5.1 0.0 copy-start.1
  5.2 0.0 copy-start.5
  5.2 2.2 %local.1 = (f32[512,128]{1,0:T(8,128)S(1)}, f32[32,128]{1,0:T(8,128)S(1)}, f32[10,32,256]{2,1,0:T(8,128)S(1)}, f32[11,32,256]{2,1,0:T(8,128)S(1)}) custom-call(f32[5,512,256]{2,1,0:T(8,128)S(1)} %bitcast.6, f32[3,512,256]{2,1,0:T(8,128)S(1)} %bitcast.9, s32[16]{0:T(128)S(1)} %copy-done.6, f32[5,256]{1,0:T(8,128)S(1)} %copy-done.4), custom_call_target="tpu_custom_call" | custom-call | flops 5000000 | bytes 5000000 | tf_op jit(solution)/shard_map/local/pallas_call | solution.py:336
  7.4 0.0 copy-start.3
  7.4 0.6 %collective-permute-start = (f32[32,128]{1,0:T(8,128)S(1)}, f32[32,128]{1,0:T(8,128)S(1)}, u32[]{:S(2)}, u32[]{:S(2)}) collective-permute-start(f32[32,128]{1,0:T(8,128)S(1)} %get-tuple-element.14), channel_id=1, source_target_pairs={{0,1},{1,0},{2,3},{3,2},{4,5},{5,4},{6,7},{7,6},{8,9},{9,8},{10,11... | collective-permute-start | bytes 49160 | tf_op jit(solution)/shard_map/ppermute | solution.py:354
  8.0 3.2 %collective-permute-done = f32[32,128]{1,0:T(8,128)S(1)} collective-permute-done((f32[32,128]{1,0:T(8,128)S(1)}, f32[32,128]{1,0:T(8,128)S(1)}, u32[]{:S(2)}, u32[]{:S(2)}) %collective-permute-start) | collective-permute-done | bytes 16416 | tf_op jit(solution)/shard_map/ppermute | solution.py:354
  11.2 1.6 %collective-permute-start.1 = (f32[1,32,128]{2,1,0:T(8,128)S(1)}, f32[1,32,128]{2,1,0:T(8,128)S(1)}, u32[]{:S(2)}, u32[]{:S(2)}) collective-permute-start(f32[1,32,128]{2,1,0:T(8,128)S(1)} %multiply_bitcast_fusion), channel_id=1, source_target_pairs={{0,2},{1,3},{2,0},{3,1},{4,6},{5,7},{6,4},{7,5},{8,10},{9,11},{10,... | collective-permute-start | bytes 49160 | tf_op jit(solution)/shard_map/ppermute | solution.py:360
  12.8 0.5 %collective-permute-start.6 = (f32[11,32,256]{2,1,0:T(8,128)S(1)}, f32[11,32,256]{2,1,0:T(8,128)S(1)}, u32[]{:S(2)}, u32[]{:S(2)}) collective-permute-start(f32[11,32,256]{2,1,0:T(8,128)S(1)} %get-tuple-element.22), channel_id=1, source_target_pairs={{1,0},{2,1},{3,2},{4,3},{5,4},{6,5},{7,6},{0,7},{9,8},{10,9},{11,1... | collective-permute-start | bytes 1081352 | tf_op jit(solution)/shard_map/ppermute | solution.py:356
  13.3 1.6 %collective-permute-done.1 = f32[1,32,128]{2,1,0:T(8,128)S(1)} collective-permute-done((f32[1,32,128]{2,1,0:T(8,128)S(1)}, f32[1,32,128]{2,1,0:T(8,128)S(1)}, u32[]{:S(2)}, u32[]{:S(2)}) %collective-permute-start.1) | collective-permute-done | bytes 16416 | tf_op jit(solution)/shard_map/ppermute | solution.py:360
  15.0 2.6 %collective-permute-start.2 = (f32[2,32,128]{2,1,0:T(8,128)S(1)}, f32[2,32,128]{2,1,0:T(8,128)S(1)}, u32[]{:S(2)}, u32[]{:S(2)}) collective-permute-start(f32[2,32,128]{2,1,0:T(8,128)S(1)} %pad_maximum_fusion.1), channel_id=1, source_target_pairs={{0,4},{1,5},{2,6},{3,7},{4,0},{5,1},{6,2},{7,3},{8,12},{9,13},{10,... | collective-permute-start | bytes 98312 | tf_op jit(solution)/shard_map/ppermute | solution.py:360
  17.6 1.5 %collective-permute-start.5 = (f32[10,32,256]{2,1,0:T(8,128)S(1)}, f32[10,32,256]{2,1,0:T(8,128)S(1)}, u32[]{:S(2)}, u32[]{:S(2)}) collective-permute-start(f32[10,32,256]{2,1,0:T(8,128)S(1)} %get-tuple-element.21), channel_id=1, source_target_pairs={{0,1},{1,2},{2,3},{3,4},{4,5},{5,6},{6,7},{7,0},{8,9},{9,10},{10,1... | collective-permute-start | bytes 983048 | tf_op jit(solution)/shard_map/ppermute | solution.py:355
  19.1 7.8 %collective-permute-done.2 = f32[2,32,128]{2,1,0:T(8,128)S(1)} collective-permute-done((f32[2,32,128]{2,1,0:T(8,128)S(1)}, f32[2,32,128]{2,1,0:T(8,128)S(1)}, u32[]{:S(2)}, u32[]{:S(2)}) %collective-permute-start.2) | collective-permute-done | bytes 32800 | tf_op jit(solution)/shard_map/ppermute | solution.py:360
  26.9 0.0 copy-done.7
  26.9 0.0 copy-done.1
  26.9 0.0 copy-done.5
  26.9 0.7 %rows.1 = (f32[32,128]{1,0:T(8,128)S(1)}, f32[32,128]{1,0:T(8,128)S(1)}, f32[10,16,256]{2,1,0:T(8,128)S(1)}, f32[11,16,256]{2,1,0:T(8,128)S(1)}) custom-call(f32[5,512,256]{2,1,0:T(8,128)S(1)} %bitcast.7, f32[3,512,256]{2,1,0:T(8,128)S(1)} %bitcast.10, s32[16]{0:T(128)S(1)} %copy-done.7, f32[5,256]{1,0:T(8,128)S(1)} %copy-done.5, ...), custom_call_target="tpu_custom_call" | custom-call | flops 2000000 | bytes 1000000 | tf_op jit(solution)/shard_map/rows/pallas_call | solution.py:363
  27.7 1.9 %collective-permute-start.4 = (f32[11,16,256]{2,1,0:T(8,128)S(1)}, f32[11,16,256]{2,1,0:T(8,128)S(1)}, u32[]{:S(2)}, u32[]{:S(2)}) collective-permute-start(f32[11,16,256]{2,1,0:T(8,128)S(1)} %get-tuple-element.18), channel_id=1, source_target_pairs={{8,0},{16,8},{24,16},{9,1},{17,9},{25,17},{10,2},{18,10},{26,18},{... | collective-permute-start | bytes 540680 | tf_op jit(solution)/shard_map/ppermute | solution.py:381
  29.6 2.4 %collective-permute-start.3 = (f32[10,16,256]{2,1,0:T(8,128)S(1)}, f32[10,16,256]{2,1,0:T(8,128)S(1)}, u32[]{:S(2)}, u32[]{:S(2)}) collective-permute-start(f32[10,16,256]{2,1,0:T(8,128)S(1)} %get-tuple-element.17), channel_id=1, source_target_pairs={{0,8},{8,16},{16,24},{1,9},{9,17},{17,25},{2,10},{10,18},{18,26},{... | collective-permute-start | bytes 491528 | tf_op jit(solution)/shard_map/ppermute | solution.py:380
  32.0 4.2 %collective-permute-done.3.up = f32[10,16,256]{2,1,0:T(8,128)S(1)} collective-permute-done((f32[10,16,256]{2,1,0:T(8,128)S(1)}, f32[10,16,256]{2,1,0:T(8,128)S(1)}, u32[]{:S(2)}, u32[]{:S(2)}) %collective-permute-start.3) | collective-permute-done | bytes 163872 | tf_op jit(solution)/shard_map/ppermute | solution.py:380
  36.3 0.0 collective-permute-done.4.dn
  36.3 0.0 copy-done.3
  36.3 13.5 %main.1 = (f32[8,512,256]{2,1,0:T(8,128)}, f32[3,512,256]{2,1,0:T(8,128)}, f32[21,32,256]{2,1,0:T(8,128)S(1)}) custom-call(f32[5,512,256]{2,1,0:T(8,128)S(1)} %bitcast.8, f32[3,512,256]{2,1,0:T(8,128)S(1)} %bitcast.11, s32[16]{0:T(128)S(1)} %copy-done.7, f32[5,256]{1,0:T(8,128)S(1)} %copy-done.5, f32[512,128]{1,0:T(8,128)S(1)} %get-tuple-element.13.q, ...), custom_call_target="tpu_custom_call" | custom-call | flops 20000000 | bytes 10000000 | tf_op jit(solution)/shard_map/main/pallas_call | solution.py:383
  49.8 0.0 collective-permute-done.5.fw
  49.8 0.0 collective-permute-done.6.bw
  49.8 1.0 %edges.1 = f32[8,32,16,256]{3,2,1,0:T(8,128)} custom-call(f32[8,32,16,256]{3,2,1,0:T(8,128)} %bitcast.12, f32[21,32,256]{2,1,0:T(8,128)S(1)} %get-tuple-element.20.e, f32[10,32,256]{2,1,0:T(8,128)S(1)} %collective-permute-done.5.fw, f32[11,32,256]{2,1,0:T(8,128)S(1)} %collective-permute-done.6.bw), custom_call_target="tpu_custom_call", output_to_operand_aliasing={{}: (0, {})} | custom-call | flops 1000000 | bytes 1000000 | tf_op jit(solution)/shard_map/edges/pallas_call | solution.py:404
  (3 shorter events, 0.0 us)
Async XLA Ops:
  0.6 26.3 %copy-start.7 = (s32[16]{0:T(128)S(1)}, s32[16]{0:T(128)}, u32[]{:S(2)}) copy-start(s32[16]{0:T(128)} %w.5) | copy-start | bytes 196
  0.6 1.7 %copy-start = (f32[5,32,16,256]{3,2,1,0:T(8,128)S(1)}, f32[5,32,16,256]{3,2,1,0:T(8,128)}, u32[]{:S(2)}) copy-start(f32[5,32,16,256]{3,2,1,0:T(8,128)} %param.4) | copy-start | bytes 7864324
  2.4 1.4 %copy-start.2 = (f32[3,32,16,256]{3,2,1,0:T(8,128)S(1)}, f32[3,32,16,256]{3,2,1,0:T(8,128)}, u32[]{:S(2)}) copy-start(f32[3,32,16,256]{3,2,1,0:T(8,128)} %param.5) | copy-start | bytes 4718596
  3.8 0.7 %copy-start.4 = (f32[5,256]{1,0:T(8,128)S(1)}, f32[5,256]{1,0:T(8,128)}, u32[]{:S(2)}) copy-start(f32[5,256]{1,0:T(8,128)} %d.5) | copy-start | bytes 15364
  4.5 0.7 %copy-start.6 = (s32[16]{0:T(128)S(1)}, s32[16]{0:T(128)}, u32[]{:S(2)}) copy-start(s32[16]{0:T(128)} %w.5) | copy-start | bytes 196
  5.1 21.8 %copy-start.1 = (f32[5,32,16,256]{3,2,1,0:T(8,128)S(1)}, f32[5,32,16,256]{3,2,1,0:T(8,128)}, u32[]{:S(2)}) copy-start(f32[5,32,16,256]{3,2,1,0:T(8,128)} %param.4) | copy-start | bytes 7864324
  5.2 21.8 %copy-start.5 = (f32[5,256]{1,0:T(8,128)S(1)}, f32[5,256]{1,0:T(8,128)}, u32[]{:S(2)}) copy-start(f32[5,256]{1,0:T(8,128)} %d.5) | copy-start | bytes 15364
  7.4 28.9 %copy-start.3 = (f32[3,32,16,256]{3,2,1,0:T(8,128)S(1)}, f32[3,32,16,256]{3,2,1,0:T(8,128)}, u32[]{:S(2)}) copy-start(f32[3,32,16,256]{3,2,1,0:T(8,128)} %param.5) | copy-start | bytes 4718596
  7.4 3.8 %collective-permute-start = (f32[32,128]{1,0:T(8,128)S(1)}, f32[32,128]{1,0:T(8,128)S(1)}, u32[]{:S(2)}, u32[]{:S(2)}) collective-permute-start(f32[32,128]{1,0:T(8,128)S(1)} %get-tuple-element.14), channel_id=1, source_target_pairs={{0,1},{1,0},{2,3},{3,2},{4,5},{5,4},{6,7},{7,6},{8,9},{9,8},{10,11... | collective-permute-start | bytes 49160 | tf_op jit(solution)/shard_map/ppermute | solution.py:354
  11.2 3.7 %collective-permute-start.1 = (f32[1,32,128]{2,1,0:T(8,128)S(1)}, f32[1,32,128]{2,1,0:T(8,128)S(1)}, u32[]{:S(2)}, u32[]{:S(2)}) collective-permute-start(f32[1,32,128]{2,1,0:T(8,128)S(1)} %multiply_bitcast_fusion), channel_id=1, source_target_pairs={{0,2},{1,3},{2,0},{3,1},{4,6},{5,7},{6,4},{7,5},{8,10},{9,11},{10,... | collective-permute-start | bytes 49160 | tf_op jit(solution)/shard_map/ppermute | solution.py:360
  12.8 37.0 %collective-permute-start.6 = (f32[11,32,256]{2,1,0:T(8,128)S(1)}, f32[11,32,256]{2,1,0:T(8,128)S(1)}, u32[]{:S(2)}, u32[]{:S(2)}) collective-permute-start(f32[11,32,256]{2,1,0:T(8,128)S(1)} %get-tuple-element.22), channel_id=1, source_target_pairs={{1,0},{2,1},{3,2},{4,3},{5,4},{6,5},{7,6},{0,7},{9,8},{10,9},{11,1... | collective-permute-start | bytes 1081352 | tf_op jit(solution)/shard_map/ppermute | solution.py:356
  15.0 11.9 %collective-permute-start.2 = (f32[2,32,128]{2,1,0:T(8,128)S(1)}, f32[2,32,128]{2,1,0:T(8,128)S(1)}, u32[]{:S(2)}, u32[]{:S(2)}) collective-permute-start(f32[2,32,128]{2,1,0:T(8,128)S(1)} %pad_maximum_fusion.1), channel_id=1, source_target_pairs={{0,4},{1,5},{2,6},{3,7},{4,0},{5,1},{6,2},{7,3},{8,12},{9,13},{10,... | collective-permute-start | bytes 98312 | tf_op jit(solution)/shard_map/ppermute | solution.py:360
  17.6 32.2 %collective-permute-start.5 = (f32[10,32,256]{2,1,0:T(8,128)S(1)}, f32[10,32,256]{2,1,0:T(8,128)S(1)}, u32[]{:S(2)}, u32[]{:S(2)}) collective-permute-start(f32[10,32,256]{2,1,0:T(8,128)S(1)} %get-tuple-element.21), channel_id=1, source_target_pairs={{0,1},{1,2},{2,3},{3,4},{4,5},{5,6},{6,7},{7,0},{8,9},{9,10},{10,1... | collective-permute-start | bytes 983048 | tf_op jit(solution)/shard_map/ppermute | solution.py:355
  27.7 8.6 %collective-permute-start.4 = (f32[11,16,256]{2,1,0:T(8,128)S(1)}, f32[11,16,256]{2,1,0:T(8,128)S(1)}, u32[]{:S(2)}, u32[]{:S(2)}) collective-permute-start(f32[11,16,256]{2,1,0:T(8,128)S(1)} %get-tuple-element.18), channel_id=1, source_target_pairs={{8,0},{16,8},{24,16},{9,1},{17,9},{25,17},{10,2},{18,10},{26,18},{... | collective-permute-start | bytes 540680 | tf_op jit(solution)/shard_map/ppermute | solution.py:381
  29.6 6.6 %collective-permute-start.3 = (f32[10,16,256]{2,1,0:T(8,128)S(1)}, f32[10,16,256]{2,1,0:T(8,128)S(1)}, u32[]{:S(2)}, u32[]{:S(2)}) collective-permute-start(f32[10,16,256]{2,1,0:T(8,128)S(1)} %get-tuple-element.17), channel_id=1, source_target_pairs={{0,8},{8,16},{16,24},{1,9},{9,17},{17,25},{2,10},{10,18},{18,26},{... | collective-permute-start | bytes 491528 | tf_op jit(solution)/shard_map/ppermute | solution.py:380
